TPU v7x, 16 devices: a 4x2x1 block of a 4x4x8 slice. The times are simulated.
16 devices in a mesh: data: 2 (over y, z), seq: 8 (over x, core).
Axes of the slice: x: 4, y: 2, z: 1, core: 2. Of those that a mesh axis runs over, the one named last changes fastest.
The devices are a block of a 4x4x8 slice.
Arguments:
- act_in: bfloat16 [128, 1024, 1024], P('data', 'seq'), parts along dimension 0
- grad_out: bfloat16 [128, 1024, 1024], P('data', 'seq'), parts along dimension 0
- ln1_scale: float32 [1024], replicated
- ln1_shift: float32 [1024], replicated
- w_tok1: bfloat16 [1024, 512], replicated
- b_tok1: float32 [512], replicated
- w_tok2: bfloat16 [512, 1024], replicated
- b_tok2: float32 [1024], replicated
- ln2_scale: float32 [1024], replicated
- ln2_shift: float32 [1024], replicated
- w_chan1: bfloat16 [1024, 4096], replicated
- b_chan1: float32 [4096], replicated
- w_chan2: bfloat16 [4096, 1024], replicated
- b_chan2: float32 [1024], replicated
Outputs:
- output 1: bfloat16 [128, 1024, 1024], P('data', 'seq'), parts along dimension 0
- output 2: bfloat16 [128, 1024, 1024], P('data', 'seq'), parts along dimension 0
- output 3: float32 [2048, 512], P('data'), parts along dimension 0
- output 4: float32 [1024, 1024], P('data'), parts along dimension 0
- output 5: float32 [2048, 4096], P('data'), parts along dimension 0
- output 6: float32 [8192, 1024], P('data'), parts along dimension 0
There are 2 independent parts. A program takes and returns all parts, laid end to end along the dimension named above; an argument that names none is the same for every part.
All inputs are finite; a program needn't handle non-finite values.
Results may differ from a plain program's by a relative error of at most 0.0164204.
Values are sent between devices in bfloat16 or wider.
A program may use at most 768 MiB of HBM per device.

v0:
```python
import jax
import jax.numpy as jnp
from jax import lax
from jax.sharding import PartitionSpec as P

LN_EPS = 1e-6


def layer_norm(rows_in, ln_scale, ln_shift):
    widened = rows_in.astype(jnp.float32)
    row_mean = jnp.mean(widened, axis=-1, keepdims=True)
    centered = widened - row_mean
    row_var = jnp.mean(centered * centered, axis=-1, keepdims=True)
    return (centered * lax.rsqrt(row_var + LN_EPS) * ln_scale + ln_shift).astype(jnp.bfloat16)


def gelu_bf16(pre_act):
    return jax.nn.gelu(pre_act.astype(jnp.float32)).astype(jnp.bfloat16)


def solution(mesh):
    act_spec = P("data", "seq", None)
    part_spec = P("data", None)
    spec_in = (act_spec, act_spec) + (P(),) * 12
    spec_out = (act_spec, act_spec, part_spec, part_spec, part_spec, part_spec)

    def device_step(act_loc, grad_loc, ln1_scale, ln1_shift, w_tok1, b_tok1, w_tok2, b_tok2,
                    ln2_scale, ln2_shift, w_chan1, b_chan1, w_chan2, b_chan2):
        normed, ln1_pull = jax.vjp(lambda rows_in: layer_norm(rows_in, ln1_scale, ln1_shift), act_loc)
        normed_cols = lax.all_to_all(normed, "seq", 2, 1, tiled=True)
        tok_pre = (jnp.einsum("bsc,sd->bdc", normed_cols, w_tok1, preferred_element_type=jnp.float32)
                   + b_tok1[:, None]).astype(jnp.bfloat16)
        tok_act, tok_pull = jax.vjp(gelu_bf16, tok_pre)
        tok_cols = (jnp.einsum("bdc,ds->bsc", tok_act, w_tok2, preferred_element_type=jnp.float32)
                    + b_tok2[:, None]).astype(jnp.bfloat16)
        tok_rows = lax.all_to_all(tok_cols, "seq", 1, 2, tiled=True)
        mid_act = (act_loc.astype(jnp.float32) + tok_rows.astype(jnp.float32)).astype(jnp.bfloat16)
        normed_mid, ln2_pull = jax.vjp(lambda rows_in: layer_norm(rows_in, ln2_scale, ln2_shift), mid_act)
        chan_pre = (jnp.einsum("bsc,ch->bsh", normed_mid, w_chan1, preferred_element_type=jnp.float32)
                    + b_chan1).astype(jnp.bfloat16)
        chan_act, chan_pull = jax.vjp(gelu_bf16, chan_pre)
        chan_out = jnp.einsum("bsh,hc->bsc", chan_act, w_chan2, preferred_element_type=jnp.float32) + b_chan2
        act_out = (mid_act.astype(jnp.float32) + chan_out).astype(jnp.bfloat16)

        grad_wchan2 = jnp.einsum("bsh,bsc->hc", chan_act, grad_loc, preferred_element_type=jnp.float32)
        grad_chan_act = jnp.einsum("bsc,hc->bsh", grad_loc, w_chan2,
                                   preferred_element_type=jnp.float32).astype(jnp.bfloat16)
        (grad_chan_pre,) = chan_pull(grad_chan_act)
        grad_wchan1 = jnp.einsum("bsc,bsh->ch", normed_mid, grad_chan_pre, preferred_element_type=jnp.float32)
        grad_normed_mid = jnp.einsum("bsh,ch->bsc", grad_chan_pre, w_chan1,
                                     preferred_element_type=jnp.float32).astype(jnp.bfloat16)
        (grad_mid_ln,) = ln2_pull(grad_normed_mid)
        grad_mid = grad_loc + grad_mid_ln
        grad_mid_cols = lax.all_to_all(grad_mid, "seq", 2, 1, tiled=True)
        grad_wtok2 = jnp.einsum("bdc,bsc->ds", tok_act, grad_mid_cols, preferred_element_type=jnp.float32)
        grad_tok_act = jnp.einsum("bsc,ds->bdc", grad_mid_cols, w_tok2,
                                  preferred_element_type=jnp.float32).astype(jnp.bfloat16)
        (grad_tok_pre,) = tok_pull(grad_tok_act)
        grad_wtok1 = jnp.einsum("bsc,bdc->sd", normed_cols, grad_tok_pre, preferred_element_type=jnp.float32)
        grad_normed_cols = jnp.einsum("bdc,sd->bsc", grad_tok_pre, w_tok1,
                                      preferred_element_type=jnp.float32).astype(jnp.bfloat16)
        grad_normed = lax.all_to_all(grad_normed_cols, "seq", 1, 2, tiled=True)
        (grad_in_ln,) = ln1_pull(grad_normed)
        grad_in = grad_mid + grad_in_ln
        weight_grads = lax.psum((grad_wtok1, grad_wtok2, grad_wchan1, grad_wchan2), "seq")
        return (act_out, grad_in) + tuple(weight_grads)

    return jax.shard_map(device_step, mesh=mesh, in_specs=spec_in, out_specs=spec_out, check_vma=False)
```

profile of v0, /device:TPU:112, one launch (start us, length us, event | category | flops | bytes accessed | tf_op | source)
XLA Modules:
  0.0 1956.6 jit_solution(3580013334656153827)
XLA Ops:
  7.2 8.9 convert_reduce_fusion.1
  16.2 9.5 fusion.19
  26.9 9.5 fusion.22
  36.4 22.6 %copy.30 = bf16[64,128,1024]{1,0,2:T(8,128)(2,1)} copy(bf16[64,128,1024]{2,1,0:T(8,128)(2,1)} %fusion.22) | data formatting | bytes 33554432 | tf_op jit(solution)/shard_map/jvp()/convert_element_type | solution.py:14
  59.0 190.0 %all_to_all.54 = bf16[64,128,1024]{1,0,2:T(8,128)(2,1)S(1)} all-to-all(bf16[64,128,1024]{1,0,2:T(8,128)(2,1)} %copy.30), channel_id=1, replica_groups=mesh['data'=2,'seq'=8] {'seq'}, dimensions={2} | all-to-all | bytes 33554432 | tf_op jit(solution)/shard_map/all_to_all | solution.py:30
  249.0 36.0 %copy.57 = bf16[64,128,8,128]{1,2,3,0:T(8,128)(2,1)} copy(bf16[64,128,8,128]{1,0,3,2:T(8,128)(2,1)S(1)} %bitcast.113) | data formatting | bytes 33554432 | tf_op jit(solution)/shard_map/all_to_all | solution.py:30
  285.0 25.2 %all_to_all.43 = bf16[64,1024,128]{1,2,0:T(8,128)(2,1)} reshape(bf16[64,8,128,128]{2,1,3,0:T(8,128)(2,1)} %bitcast.114) | data formatting | bytes 33554432 | tf_op jit(solution)/shard_map/all_to_all | solution.py:30
  310.2 17.0 add_convert_fusion.4
  327.2 18.1 fusion.39
  345.3 22.6 %copy.32 = bf16[64,1024,128]{2,0,1:T(8,128)(2,1)} copy(bf16[64,1024,128]{1,2,0:T(8,128)(2,1)} %fusion.39) | data formatting | bytes 33554432 | tf_op jit(solution)/shard_map/convert_element_type | solution.py:35
  367.9 188.8 %all_to_all.55 = bf16[64,1024,128]{2,0,1:T(8,128)(2,1)S(1)} all-to-all(bf16[64,1024,128]{2,0,1:T(8,128)(2,1)} %copy.32), channel_id=1, replica_groups=mesh['data'=2,'seq'=8] {'seq'}, dimensions={1} | all-to-all | bytes 33554432 | tf_op jit(solution)/shard_map/all_to_all | solution.py:36
  556.7 36.7 %copy.55 = f32[64,8,128,128]{3,1,2,0:T(8,128)} copy(bf16[64,8,128,128]{3,0,2,1:T(8,128)(2,1)S(1)} %bitcast.112) | data formatting | bytes 50331648 | tf_op jit(solution)/shard_map/convert_element_type | solution.py:37
  593.3 35.4 %reshape.76 = f32[64,128,1024]{2,1,0:T(8,128)} reshape(f32[64,128,8,128]{3,2,1,0:T(8,128)} %bitcast.110) | data formatting | bytes 67108864 | tf_op jit(solution)/shard_map/convert_element_type | solution.py:37
  628.8 16.2 convert_reduce_fusion
  645.1 6.1 copy-done.2
  651.2 5.6 fusion.25
  657.5 79.9 %add_convert_fusion = bf16[64,128,4096]{2,1,0:T(8,128)(2,1)} fusion(f32[4096]{0:T(1024)S(1)} %copy-done.22, bf16[64,128,1024]{2,1,0:T(8,128)(2,1)} %copy-done.2, f32[1024]{0:T(1024)S(1)} %copy-done.24, f32[1024]{0:T(1024)S(1)} %copy-done.17, f32[64,128]{1,0:T(8,128)S(1)} %fusion.62, f32[64,128]{1,0:T(8,128)S(1)} %broadcast_multiply_fusion, ...), kind=kOutput, calls=%fused_computation.17 | convolution fusion | flops 68836917248 | bytes 92364800 | tf_op jit(solution)/shard_map/bsc,ch->bsh/dot_general | solution.py:39
  737.4 150.0 %fusion.3 = bf16[64,128,4096]{2,1,0:T(8,128)(2,1)} fusion(bf16[64,128,4096]{2,1,0:T(8,128)(2,1)} %add_convert_fusion, bf16[64,128,1024]{2,1,0:T(8,128)(2,1)} %param.15, bf16[4096,1024]{1,0:T(8,128)(2,1)} %param.26), kind=kOutput, calls=%fused_computation.9 | convolution fusion | flops 69491228672 | bytes 159383552 | tf_op jit(solution)/shard_map/bsc,hc->bsh/dot_general | solution.py:46
  887.4 81.1 %fusion.29 = (f32[64,128]{1,0:T(8,128)S(1)}, bf16[64,128,1024]{2,1,0:T(8,128)(2,1)}) fusion(bf16[64,128,1024]{2,1,0:T(8,128)(2,1)} %copy-done.2, f32[1024]{0:T(1024)S(1)} %copy-done.18, f32[64,128]{1,0:T(8,128)} %copy-done.7, bf16[64,128,4096]{2,1,0:T(8,128)(2,1)} %fusion.3, bf16[1024,4096]{1,0:T(8,128)(2,1)} %param.24), kind=kOutput, calls=%fused_computation.44 | convolution fusion | flops 68778188800 | bytes 109121536 | tf_op jit(solution)/shard_map/bsh,ch->bsc/dot_general | solution.py:50
  968.6 16.5 fusion.31
  985.1 26.4 %fusion.40 = bf16[64,128,1024]{2,1,0:T(8,128)(2,1)} fusion(bf16[64,128,1024]{2,1,0:T(8,128)(2,1)} %param.15, bf16[64,128,1024]{2,1,0:T(8,128)(2,1)} %copy-done.2, bf16[64,128,1024]{2,1,0:T(8,128)(2,1)} %get-tuple-element.13, f32[64,128]{1,0:T(8,128)S(1)} %negate_multiply_fusion.1, f32[64,128]{1,0:T(8,128)S(1)} %multiply_multiply_fusion.3, ...), kind=kLoop, calls=%fused_computation.63 | loop fusion | flops 92274688 | bytes 67244032 | tf_op jit(solution)/shard_map/add | solution.py:53
  1011.5 22.6 %copy.34 = bf16[64,128,1024]{1,0,2:T(8,128)(2,1)} copy(bf16[64,128,1024]{2,1,0:T(8,128)(2,1)} %fusion.40) | data formatting | bytes 33554432 | tf_op jit(solution)/shard_map/add | solution.py:53
  1034.1 6.1 all-to-all-start.2
  1040.2 83.9 %fusion.50 = f32[1024,4096]{1,0:T(8,128)} fusion(bf16[64,128,4096]{2,1,0:T(8,128)(2,1)} %fusion.3, bf16[64,128,1024]{2,1,0:T(8,128)(2,1)} %copy-done.2, f32[1024]{0:T(1024)S(1)} %copy-done.25, f32[1024]{0:T(1024)S(1)} %copy-done.18, f32[64,128]{1,0:T(8,128)S(1)} %copy-done.14, f32[64,128]{1,0:T(8,128)S(1)} %copy-done.8), kind=kOutput, calls=%fused_computation.80 | convolution fusion | flops 68769808384 | bytes 100737024 | tf_op jit(solution)/shard_map/bsc,bsh->ch/dot_general | solution.py:49
  1124.1 82.3 %convolution_bitcast_fusion = f32[4096,1024]{1,0:T(8,128)} fusion(bf16[64,128,1024]{2,1,0:T(8,128)(2,1)} %param.15, bf16[64,128,4096]{2,1,0:T(8,128)(2,1)} %add_convert_fusion), kind=kOutput, calls=%fused_computation.79 | convolution fusion | flops 69055021056 | bytes 100663296 | tf_op jit(solution)/shard_map/bsh,bsc->hc/dot_general | solution.py:45
  1206.3 18.1 all-to-all-done.2
  1224.5 18.5 copy.56
  1243.0 25.3 %all_to_all.48 = bf16[64,1024,128]{1,2,0:T(8,128)(2,1)} reshape(bf16[64,8,128,128]{2,1,3,0:T(8,128)(2,1)} %bitcast.115) | data formatting | bytes 33554432 | tf_op jit(solution)/shard_map/all_to_all | solution.py:54
  1268.3 18.3 convolution_bitcast_fusion.1
  1286.6 26.1 %fusion.38 = bf16[64,512,128]{1,2,0:T(8,128)(2,1)} fusion(bf16[64,128,512]{2,1,0:T(8,128)(2,1)} %add_convert_fusion.4, bf16[64,1024,128]{1,2,0:T(8,128)(2,1)} %all_to_all.48, bf16[512,1024]{1,0:T(8,128)(2,1)S(1)} %copy-done), kind=kOutput, calls=%fused_computation.61 | convolution fusion | flops 8686403584 | bytes 34603008 | tf_op jit(solution)/shard_map/bsc,ds->bdc/dot_general | solution.py:56
  1312.7 16.0 convolution_bitcast_fusion.2
  1328.7 15.9 convert_bitcast_fusion
  1344.6 22.7 %copy.36 = bf16[64,1024,128]{2,0,1:T(8,128)(2,1)} copy(bf16[64,1024,128]{1,2,0:T(8,128)(2,1)} %convert_bitcast_fusion) | data formatting | bytes 33554432 | tf_op jit(solution)/shard_map/convert_element_type | solution.py:61
  1367.3 6.0 all-to-all-start.3
  1374.1 92.8 %fusion.30 = bf16[64,128,1024]{2,1,0:T(8,128)(2,1)} fusion(bf16[64,128,1024]{2,1,0:T(8,128)(2,1)} %copy-done.2, f32[1024]{0:T(1024)S(1)} %copy-done.26, bf16[4096,1024]{1,0:T(8,128)(2,1)} %param.26, bf16[64,128,4096]{2,1,0:T(8,128)(2,1)} %add_convert_fusion), kind=kOutput, calls=%fused_computation.45 | convolution fusion | flops 69088575488 | bytes 109056000 | tf_op jit(solution)/shard_map/bsh,hc->bsc/dot_general | solution.py:42
  1466.9 175.8 %all-to-all-done.3 = bf16[64,1024,128]{2,0,1:T(8,128)(2,1)} async-done(((bf16[64,1024,128]{2,0,1:T(8,128)(2,1)}), bf16[64,1024,128]{2,0,1:T(8,128)(2,1)}, u32[]{:S(2)}, u32[]{:S(2)}) %all-to-all-start.3) | async-done | bytes 16777248 | tf_op jit(solution)/shard_map/all_to_all | solution.py:62
  1642.7 21.8 %copy.54 = f32[64,8,128,128]{3,1,2,0:T(8,128)} copy(bf16[64,8,128,128]{3,0,2,1:T(8,128)(2,1)} %bitcast.21) | data formatting | bytes 50331648 | tf_op jit(solution)/shard_map/transpose(jvp())/convert_element_type | solution.py:14
  1664.5 35.5 %reshape.77 = f32[64,128,1024]{2,1,0:T(8,128)} reshape(f32[64,128,8,128]{3,2,1,0:T(8,128)} %bitcast.111) | data formatting | bytes 67108864 | tf_op jit(solution)/shard_map/transpose(jvp())/convert_element_type | solution.py:14
  1700.0 20.8 %fusion.23 = f32[64,128]{1,0:T(8,128)S(1)} fusion(bf16[64,128,1024]{2,1,0:T(8,128)(2,1)} %param.14, f32[64,128,1024]{2,1,0:T(8,128)} %reshape.77, f32[1024]{0:T(1024)S(1)} %copy-done.16, f32[64,128]{1,0:T(8,128)S(1)} %copy-done.4), kind=kLoop, calls=%fused_computation.38 | loop fusion | flops 41934848 | bytes 50401280 | tf_op jit(solution)/shard_map/transpose(jvp())/reduce_sum | solution.py:14
  1720.9 4.1 copy-done.1
  1725.0 13.3 fusion.46
  1738.4 28.0 %fusion.41 = bf16[64,128,1024]{2,1,0:T(8,128)(2,1)} fusion(bf16[64,128,1024]{2,1,0:T(8,128)(2,1)} %fusion.40, f32[64,128]{1,0:T(8,128)S(1)} %negate_multiply_fusion, f32[64,128]{1,0:T(8,128)S(1)} %multiply_multiply_fusion.2, f32[64,128]{1,0:T(8,128)S(1)} %copy-done.4, bf16[64,128,1024]{2,1,0:T(8,128)(2,1)} %param.14, f32[64,128]{1,0:T(8,128)S(1)} %copy-done.6, ...), kind=kLoop, calls=%fused_computation.64 | loop fusion | flops 83886080 | bytes 84021248 | tf_op jit(solution)/shard_map/add | solution.py:64
  1766.3 155.3 %all-reduce.3.cloned.1.call-done = (f32[1024,512]{1,0:T(8,128)}, f32[512,1024]{1,0:T(8,128)}, f32[1024,4096]{1,0:T(8,128)}, f32[4096,1024]{1,0:T(8,128)}) async-done(((f32[1024,512]{1,0:T(8,128)}, f32[512,1024]{1,0:T(8,128)}, f32[1024,4096]{1,0:T(8,128)}, f32[4096,1024]{1,0:T(8,128)}), (f32[1024,512]{1,0:T(8,128)}, f32[512,1024]{1,0:T(8,128)}, f32[1024,4096]{1,0:T(8,128)}, ...) | async-done | bytes 37748752 | tf_op jit(solution)/shard_map/psum | solution.py:65
  1921.6 3.2 copy.62
  1924.8 3.2 copy.63
  1928.0 13.5 copy.64
  1941.5 1.8 slice-done.7
  1943.3 6.2 copy.65
  (81 shorter events, 2.8 us)
Async XLA Ops:
  7.2 320.1 %copy-start = (bf16[512,1024]{1,0:T(8,128)(2,1)S(1)}, bf16[512,1024]{1,0:T(8,128)(2,1)}, u32[]{:S(2)}) copy-start(bf16[512,1024]{1,0:T(8,128)(2,1)} %param.20) | copy-start | bytes 3145732
  7.2 19.7 %slice-start = ((s8[16777216]{0:T(1024)(128)(4,1)}), s8[4194304]{0:T(1024)(128)(4,1)S(1)}, s32[]{:S(2)}) async-start(s8[16777216]{0:T(1024)(128)(4,1)} %bitcast.108), calls=%async_computation.5 | async-start | bytes 8388608
  7.2 19.7 %slice-start.1 = ((s8[16777216]{0:T(1024)(128)(4,1)}), s8[4194304]{0:T(1024)(128)(4,1)S(1)}, s32[]{:S(2)}) async-start(s8[16777216]{0:T(1024)(128)(4,1)} %bitcast.108), calls=%async_computation.6 | async-start | bytes 8388608
  7.2 19.7 %copy-start.15 = (f32[1024]{0:T(1024)S(1)}, f32[1024]{0:T(1024)}, u32[]{:S(2)}) copy-start(f32[1024]{0:T(1024)} %param.16) | copy-start | bytes 12292
  7.2 19.7 %copy-start.19 = (f32[1024]{0:T(1024)S(1)}, f32[1024]{0:T(1024)}, u32[]{:S(2)}) copy-start(f32[1024]{0:T(1024)} %param.17) | copy-start | bytes 12292
  16.1 10.2 copy-start.3
  16.1 10.8 slice-start.2
  16.2 10.8 slice-start.3
  25.7 0.6 copy-start.9
  26.3 0.6 copy-start.5
  249.0 61.2 %copy-start.20 = (bf16[1024,512]{1,0:T(8,128)(2,1)S(1)}, bf16[1024,512]{1,0:T(8,128)(2,1)}, u32[]{:S(2)}) copy-start(bf16[1024,512]{1,0:T(8,128)(2,1)} %param.18) | copy-start | bytes 3145732
  249.0 61.2 %copy-start.27 = (f32[512]{0:T(512)S(1)}, f32[512]{0:T(512)}, u32[]{:S(2)}) copy-start(f32[512]{0:T(512)} %param.19) | copy-start | bytes 6148
  310.2 17.0 copy-start.23
  628.8 28.7 %copy-start.17 = (f32[1024]{0:T(1024)S(1)}, f32[1024]{0:T(1024)}, u32[]{:S(2)}) copy-start(f32[1024]{0:T(1024)} %param.22) | copy-start | bytes 12292
  628.8 28.7 %copy-start.22 = (f32[4096]{0:T(1024)S(1)}, f32[4096]{0:T(1024)}, u32[]{:S(2)}) copy-start(f32[4096]{0:T(1024)} %param.25) | copy-start | bytes 49156
  628.8 28.7 %copy-start.24 = (f32[1024]{0:T(1024)S(1)}, f32[1024]{0:T(1024)}, u32[]{:S(2)}) copy-start(f32[1024]{0:T(1024)} %param.23) | copy-start | bytes 12292
  645.0 6.2 copy-start.2
  645.0 92.3 %copy-start.7 = (f32[64,128]{1,0:T(8,128)}, f32[64,128]{1,0:T(8,128)S(1)}, u32[]{:S(2)}) copy-start(f32[64,128]{1,0:T(8,128)S(1)} %broadcast_multiply_fusion) | copy-start | bytes 98308
  656.8 0.6 copy-start.11
  657.5 79.9 %copy-start.13 = (f32[64,128]{1,0:T(8,128)}, f32[64,128]{1,0:T(8,128)S(1)}, u32[]{:S(2)}) copy-start(f32[64,128]{1,0:T(8,128)S(1)} %fusion.62) | copy-start | bytes 98308
  737.4 150.0 %copy-start.18 = (f32[1024]{0:T(1024)S(1)}, f32[1024]{0:T(1024)}, u32[]{:S(2)}) copy-start(f32[1024]{0:T(1024)} %param.22) | copy-start | bytes 12292
  887.4 81.2 %copy-start.12 = (f32[64,128]{1,0:T(8,128)S(1)}, f32[64,128]{1,0:T(8,128)}, u32[]{:S(2)}) copy-start(f32[64,128]{1,0:T(8,128)} %copy-done.11) | copy-start | bytes 98308
  887.4 81.2 %copy-start.8 = (f32[64,128]{1,0:T(8,128)S(1)}, f32[64,128]{1,0:T(8,128)}, u32[]{:S(2)}) copy-start(f32[64,128]{1,0:T(8,128)} %copy-done.7) | copy-start | bytes 98308
  887.4 81.2 %copy-start.14 = (f32[64,128]{1,0:T(8,128)S(1)}, f32[64,128]{1,0:T(8,128)}, u32[]{:S(2)}) copy-start(f32[64,128]{1,0:T(8,128)} %copy-done.13) | copy-start | bytes 98308
  1011.5 28.7 %copy-start.25 = (f32[1024]{0:T(1024)S(1)}, f32[1024]{0:T(1024)}, u32[]{:S(2)}) copy-start(f32[1024]{0:T(1024)} %param.23) | copy-start | bytes 12292
  1034.1 190.4 %all-to-all-start.2 = ((bf16[64,128,1024]{1,0,2:T(8,128)(2,1)}), bf16[64,128,1024]{1,0,2:T(8,128)(2,1)}, u32[]{:S(2)}, u32[]{:S(2)}) async-start(bf16[64,128,1024]{1,0,2:T(8,128)(2,1)} %copy.34), calls=%async_computation.2 | async-start | bytes 33554432 | tf_op jit(solution)/shard_map/all_to_all | solution.py:54
  1312.7 16.0 copy-start.21
  1367.3 6.8 copy-start.26
  1367.3 275.4 %all-to-all-start.3 = ((bf16[64,1024,128]{2,0,1:T(8,128)(2,1)}), bf16[64,1024,128]{2,0,1:T(8,128)(2,1)}, u32[]{:S(2)}, u32[]{:S(2)}) async-start(bf16[64,1024,128]{2,0,1:T(8,128)(2,1)} %copy.36), calls=%async_computation.3 | async-start | bytes 33554432 | tf_op jit(solution)/shard_map/all_to_all | solution.py:62
  1373.3 548.3 %all-reduce.3.cloned.1.call-start = ((), (), s32[]{:S(2)}) async-start(), calls=%async_computation.4 | async-start | bytes 75497472 | tf_op jit(solution)/shard_map/psum | solution.py:65
  1664.5 35.5 %copy-start.4 = (f32[64,128]{1,0:T(8,128)S(1)}, f32[64,128]{1,0:T(8,128)}, u32[]{:S(2)}) copy-start(f32[64,128]{1,0:T(8,128)} %copy-done.3) | copy-start | bytes 98308
  1664.5 35.5 %copy-start.16 = (f32[1024]{0:T(1024)S(1)}, f32[1024]{0:T(1024)}, u32[]{:S(2)}) copy-start(f32[1024]{0:T(1024)} %param.16) | copy-start | bytes 12292
  1700.0 20.8 %copy-start.10 = (f32[64,128]{1,0:T(8,128)S(1)}, f32[64,128]{1,0:T(8,128)}, u32[]{:S(2)}) copy-start(f32[64,128]{1,0:T(8,128)} %copy-done.9) | copy-start | bytes 98308
  1700.0 25.0 %copy-start.1 = (f32[64,128,1024]{2,1,0:T(8,128)S(1)}, f32[64,128,1024]{2,1,0:T(8,128)}, u32[]{:S(2)}) copy-start(f32[64,128,1024]{2,1,0:T(8,128)} %reshape.77) | copy-start | bytes 100663296
  1700.0 25.0 %copy-start.6 = (f32[64,128]{1,0:T(8,128)S(1)}, f32[64,128]{1,0:T(8,128)}, u32[]{:S(2)}) copy-start(f32[64,128]{1,0:T(8,128)} %copy-done.5) | copy-start | bytes 98308
  1921.6 19.9 %slice-start.4 = ((s8[16777216]{0:T(1024)(128)(4,1)}), s8[4194304]{0:T(1024)(128)(4,1)S(1)}, s32[]{:S(2)}) async-start(s8[16777216]{0:T(1024)(128)(4,1)} %bitcast.116), calls=%async_computation.9 | async-start | bytes 8388608
  1928.0 13.5 slice-start.5
  1928.0 13.5 slice-start.6
  1928.0 15.3 slice-start.7
Sparse Core Ops, SparseCore 0:
  1377.6 543.9 all-reduce.2
where the time goes:
time: 1970 us; the launch traced here: 1960 us
  matrix products  681 us (35%)
  blocking collectives  379 us (19%)
  local copies, waits for them, and re-layouts  365 us (19%)
  waiting for transfers between devices  350 us (18%)
  other arithmetic  155 us (8%)
    all_to_all x1, blocking collectives, device_step(): normed_cols = lax.all_to_all(normed, 'seq', 2, 1, tiled=True)  190 us
    all_to_all x1, blocking collectives, device_step(): tok_rows = lax.all_to_all(tok_cols, 'seq', 1, 2, tiled=True)  189 us
    all_to_all x1, waiting for transfers between devices, device_step(): grad_normed = lax.all_to_all(grad_normed_cols, 'seq', 1, 2, tiled=True)  176 us
    psum x1, waiting for transfers between devices, device_step(): lax.psum((grad_wtok1, grad_wtok2, grad_wchan1, grad_wchan2), 'seq')  155 us
    dot_general x1, matrix products, device_step(): jnp.einsum('bsc,hc->bsh', grad_loc, w_chan2, preferred_element_type=jnp.f...  150 us
    dot_general x1, matrix products, device_step(): jnp.einsum('bsh,hc->bsc', chan_act, w_chan2, preferred_element_type=jnp.f...  92.8 us
    dot_general x1, matrix products, device_step(): jnp.einsum('bsc,bsh->ch', normed_mid, grad_chan_pre, preferred_element_ty...  83.9 us
    dot_general x1, matrix products, device_step(): jnp.einsum('bsh,bsc->hc', chan_act, grad_loc, preferred_element_type=jnp....  82.3 us
  transfers between devices with their start and end apart: 3, of which 3 were waited for; matrix products, arithmetic and copies ran while one was open for 19% of the time, Pallas kernels for 0%

commit v1 on v0

v1 whole, which is shorter than its diff:
```python
import functools
import math

import jax
import jax.numpy as jnp
from jax import lax
from jax.experimental import pallas as pl
from jax.experimental.pallas import tpu as pltpu
from jax.sharding import PartitionSpec as P

LN_EPS = 1e-6
GELU_C = math.sqrt(2.0 / math.pi)
F32, BF16 = jnp.float32, jnp.bfloat16
AHEAD = 3
ROWS_LN = 32
TILE = 512


def dot(a, b):
    return jnp.dot(a, b, preferred_element_type=F32)


def dot_nt(a, b):
    return lax.dot_general(a, b, (((1,), (1,)), ((), ())), preferred_element_type=F32)


def gelu(x):
    th = jnp.tanh(GELU_C * (x + 0.044715 * (x * x * x)))
    return 0.5 * x * (1.0 + th)


def gelu_and_slope(x):
    sq = x * x
    th = jnp.tanh(x * (GELU_C + (GELU_C * 0.044715) * sq))
    half = 0.5 + 0.5 * th
    slope = half + (0.5 * x) * (1.0 - th * th) * (GELU_C + (3.0 * 0.044715 * GELU_C) * sq)
    return x * half, slope


def normalize(rows_in):
    mean = jnp.mean(rows_in, axis=-1, keepdims=True)
    centered = rows_in - mean
    inv = lax.rsqrt(jnp.mean(centered * centered, axis=-1, keepdims=True) + LN_EPS)
    return centered * inv, inv


def norm_grad(unit, inv, scaled):
    return inv * (scaled - jnp.mean(scaled, axis=-1, keepdims=True)
                  - unit * jnp.mean(scaled * unit, axis=-1, keepdims=True))


def layer_kernel(n, x_hbm, dz_hbm, s1, o1, s2, o2, bt1, bt2, b1_ref, b2_ref, wt1, wt1_t, wt2, wt2_t, wc1, wc2, eye,
                 z_out, dx_out, dw1_hbm, dw2_hbm, dwt1, dwt2, xg, dzg, zg, dxg,
                 xv, dzv, x1, v, h, g, vt, dzt, zacc, dvacc, q, da, w1s, w2s, d1s, d2s,
                 send_in, send_out, recv_x, recv_dz, recv_z, recv_dx, load_x, load_dz, store, own_out, wsem, dsem_in, dsem_out):
    me = lax.axis_index("seq")
    own, rows, chans = x_hbm.shape[0] // n, x_hbm.shape[1], x_hbm.shape[2]
    patches = n * rows
    hid_tok = h.shape[0]
    hid = wc1.shape[1]
    block = w1s.shape[2]
    blocks = hid // block
    steps = own * blocks

    def peer(k):
        return lax.rem(me + k, n)

    def rsl(i, size):
        return pl.ds(pl.multiple_of(i * size, size), size)

    barrier = pltpu.get_barrier_semaphore()
    for k in range(1, n):
        pl.semaphore_signal(barrier, inc=1, device_id={"seq": peer(k)}, device_id_type=pl.DeviceIdType.MESH)
    pl.semaphore_wait(barrier, n - 1)

    def send_image(i):
        for src, dst, recv, idx in ((x_hbm, xg, recv_x, 0), (dz_hbm, dzg, recv_dz, 1)):
            for k in range(1, n):
                p = peer(k)
                pltpu.make_async_remote_copy(
                    src_ref=src.at[p * own + i], dst_ref=dst.at[i, me], send_sem=send_in.at[idx], recv_sem=recv.at[i],
                    device_id={"seq": p}, device_id_type=pl.DeviceIdType.MESH).start()

    def send_result(i):
        for src, dst, recv, idx in ((zg, z_out, recv_z, 0), (dxg, dx_out, recv_dx, 1)):
            for k in range(1, n):
                p = peer(k)
                pltpu.make_async_remote_copy(
                    src_ref=src.at[i, p], dst_ref=dst.at[me * own + i], send_sem=send_out.at[idx], recv_sem=recv.at[0],
                    device_id={"seq": p}, device_id_type=pl.DeviceIdType.MESH).start()

    def wait_bytes(ref, sem):
        pltpu.make_async_copy(ref, ref, sem).wait()

    def load_image(i, src, gathered, buf, recv, sem):
        wait_bytes(gathered.at[0, pl.ds(0, n - 1)], recv.at[i])
        for k in range(n):
            p = peer(k)
            ref = src.at[me * own + i] if k == 0 else gathered.at[i, p]
            pltpu.make_async_copy(ref, buf.at[rsl(p, rows)], sem).start()

    def weight_copies(t):
        j, slot = lax.rem(t, blocks), lax.rem(t, 2)
        return (pltpu.make_async_copy(wc1.at[:, rsl(j, block)], w1s.at[slot], wsem.at[0, slot]),
                pltpu.make_async_copy(wc2.at[rsl(j, block)], w2s.at[slot], wsem.at[1, slot]))

    def grad_refs(t):
        j, slot = lax.rem(t, blocks), lax.rem(t, 3)
        return ((dw1_hbm.at[:, rsl(j, block)], d1s.at[slot]), (dw2_hbm.at[:, rsl(j, block)], d2s.at[slot]))

    def grad_in(t):
        return [pltpu.make_async_copy(a, b, dsem_in.at[m, lax.rem(t, 3)]) for m, (a, b) in enumerate(grad_refs(t))]

    def grad_out(t):
        return [pltpu.make_async_copy(b, a, dsem_out.at[m, lax.rem(t, 3)]) for m, (a, b) in enumerate(grad_refs(t))]

    def result_copies(i):
        out = []
        for m, (buf, staged, final) in enumerate(((x1, zg, z_out), (dzt, dxg, dx_out))):
            out.append(pltpu.make_async_copy(buf.at[rsl(me, rows)], final.at[me * own + i], own_out.at[m]))
            for k in range(1, n):
                p = peer(k)
                out.append(pltpu.make_async_copy(buf.at[rsl(p, rows)], staged.at[i, p], store.at[m]))
        return out

    def wait_results():
        for m in range(2):
            wait_bytes(zg.at[0, pl.ds(0, n - 1)], store.at[m])
            wait_bytes(zg.at[0, 0], own_out.at[m])

    for i in range(min(AHEAD, own)):
        send_image(i)
    for c in weight_copies(0):
        c.start()
    dwt1[...] = jnp.zeros_like(dwt1)
    dwt2[...] = jnp.zeros_like(dwt2)
    load_image(0, x_hbm, xg, xv.at[0], recv_x, load_x.at[0])

    def image_step(i, carry):
        slot = lax.rem(i, 2)
        xi = xv.at[slot]

        @pl.when(i + AHEAD < own)
        def _():
            send_image(i + AHEAD)

        @pl.when(i > 0)
        def _():
            wait_results()
            send_result(i - 1)

        wait_bytes(xi, load_x.at[slot])

        def ln1_rows(r, c):
            sl = rsl(r, ROWS_LN)
            unit, _ = normalize(xi[sl].astype(F32))
            vt[sl] = (unit * s1[...] + o1[...]).astype(BF16)
            return c

        lax.fori_loop(0, patches // ROWS_LN, ln1_rows, 0)

        def tok_hidden(ct, c):
            sl = rsl(ct, TILE)
            pre = (dot(wt1_t[...], vt[:, sl]) + bt1[...]).astype(BF16)
            h[:, sl] = pre
            g[:, sl] = gelu(pre.astype(F32)).astype(BF16)
            return c

        lax.fori_loop(0, chans // TILE, tok_hidden, 0)
        load_image(i, dz_hbm, dzg, dzv, recv_dz, load_dz)

        def tok_out(rt, c):
            sl = rsl(rt, TILE)
            t = (dot(wt2_t[sl], g[...]) + bt2[sl]).astype(BF16)
            mid = (xi[sl].astype(F32) + t.astype(F32)).astype(BF16)
            x1[sl] = mid
            return c

        lax.fori_loop(0, patches // TILE, tok_out, 0)

        def ln2_rows(r, c):
            sl = rsl(r, ROWS_LN)
            mid = x1[sl].astype(F32)
            unit, _ = normalize(mid)
            v[sl] = (unit * s2[...] + o2[...]).astype(BF16)
            zacc[sl] = mid + b2_ref[...]
            dvacc[sl] = jnp.zeros_like(mid)
            return c

        lax.fori_loop(0, patches // ROWS_LN, ln2_rows, 0)
        wait_bytes(dzv, load_dz)

        def flip(ct, c):
            sl = rsl(ct, 256)
            vt[sl] = dot_nt(eye[...], v[:, sl]).astype(BF16)
            dzt[sl] = dot_nt(eye[...], dzv[:, sl]).astype(BF16)
            return c

        lax.fori_loop(0, chans // 256, flip, 0)

        def chan_step(j, c):
            t = i * blocks + j
            ws, ds = lax.rem(t, 2), lax.rem(t, 3)
            for cp in weight_copies(t):
                cp.wait()

            @pl.when(t + 1 < steps)
            def _():
                for cp in weight_copies(t + 1):
                    cp.start()

            @pl.when(t >= 2)
            def _():
                for cp in grad_out(t - 2):
                    cp.wait()

            @pl.when(jnp.logical_and(t + 1 >= blocks, t + 1 < steps))
            def _():
                for cp in grad_in(t + 1):
                    cp.start()

            bias = b1_ref[:, rsl(j, block)]

            def rows_step(rt, c2):
                sl = rsl(rt, TILE)
                a = (dot(v[sl], w1s[ws]) + bias).astype(BF16)
                act, slope = gelu_and_slope(a.astype(F32))
                act = act.astype(BF16)
                q[sl] = act
                dq = dot_nt(dzv[sl], w2s[ws]).astype(BF16)
                grad = (dq.astype(F32) * slope).astype(BF16)
                da[sl] = grad
                zacc[sl] += dot(act, w2s[ws])
                dvacc[sl] += dot_nt(grad, w1s[ws])
                return c2

            lax.fori_loop(0, patches // TILE, rows_step, 0)

            @pl.when(i == 0)
            def _():
                d1s[ds] = jnp.zeros(d1s.shape[1:], F32)
                d2s[ds] = jnp.zeros(d2s.shape[1:], F32)

            @pl.when(i > 0)
            def _():
                for cp in grad_in(t):
                    cp.wait()

            def weights_step(rt, c2):
                sl = rsl(rt, TILE)
                d1s[ds, sl] += dot(vt[sl], da[...])
                d2s[ds, sl] += dot(dzt[sl], q[...])
                return c2

            lax.fori_loop(0, chans // TILE, weights_step, 0)
            for cp in grad_out(t):
                cp.start()
            return c

        lax.fori_loop(0, blocks, chan_step, 0)

        @pl.when(i + 1 < own)
        def _():
            load_image(i + 1, x_hbm, xg, xv.at[1 - slot], recv_x, load_x.at[1 - slot])

        def ln2_grad(r, c):
            sl = rsl(r, ROWS_LN)
            unit, inv = normalize(x1[sl].astype(F32))
            scaled = dvacc[sl].astype(BF16).astype(F32) * s2[...]
            through = norm_grad(unit, inv, scaled).astype(BF16)
            v[sl] = (dzv[sl].astype(F32) + through.astype(F32)).astype(BF16)
            x1[sl] = zacc[sl].astype(BF16)
            unit1, _ = normalize(xi[sl].astype(F32))
            vt[sl] = (unit1 * s1[...] + o1[...]).astype(BF16)
            return c

        lax.fori_loop(0, patches // ROWS_LN, ln2_grad, 0)

        def tok_hidden_grad(ct, c):
            sl = rsl(ct, TILE)
            dg = dot(wt2[...], v[:, sl]).astype(BF16)
            _, slope = gelu_and_slope(h[:, sl].astype(F32))
            h[:, sl] = (dg.astype(F32) * slope).astype(BF16)
            return c

        lax.fori_loop(0, chans // TILE, tok_hidden_grad, 0)

        def tok_weights(rt, c):
            sl = rsl(rt, TILE)
            dwt1[sl] += dot_nt(vt[sl], h[...])
            dwt2[:, sl] += dot_nt(g[...], v[sl])
            return c

        lax.fori_loop(0, patches // TILE, tok_weights, 0)

        def tok_in_grad(rt, c):
            sl = rsl(rt, TILE)
            vt[sl] = dot(wt1[sl], h[...]).astype(BF16)
            return c

        lax.fori_loop(0, patches // TILE, tok_in_grad, 0)

        def ln1_grad(r, c):
            sl = rsl(r, ROWS_LN)
            unit, inv = normalize(xi[sl].astype(F32))
            through = norm_grad(unit, inv, vt[sl].astype(F32) * s1[...]).astype(BF16)
            dzt[sl] = (v[sl].astype(F32) + through.astype(F32)).astype(BF16)
            return c

        lax.fori_loop(0, patches // ROWS_LN, ln1_grad, 0)
        for cp in result_copies(i):
            cp.start()
        return carry

    lax.fori_loop(0, own, image_step, 0)
    for t in (steps - 2, steps - 1):
        for cp in grad_out(t):
            cp.wait()
    wait_results()
    send_result(own - 1)
    for m in range(2):
        wait_bytes(xg.at[:, pl.ds(0, n - 1)], send_in.at[m])
        wait_bytes(xg.at[:, pl.ds(0, n - 1)], send_out.at[m])
    wait_bytes(xg.at[:, pl.ds(0, n - 1)], recv_z.at[0])
    wait_bytes(xg.at[:, pl.ds(0, n - 1)], recv_dx.at[0])


def solution(mesh):
    act_spec = P("data", "seq", None)
    part_spec = P("data", None)
    spec_in = (act_spec, act_spec) + (P(),) * 12
    spec_out = (act_spec, act_spec, part_spec, part_spec, part_spec, part_spec)
    n = mesh.shape["seq"]

    def device_step(act_loc, grad_loc, ln1_scale, ln1_shift, w_tok1, b_tok1, w_tok2, b_tok2,
                    ln2_scale, ln2_shift, w_chan1, b_chan1, w_chan2, b_chan2):
        images, rows, chans = act_loc.shape
        own, patches = images // n, rows * n
        hid_tok, hid = w_tok1.shape[1], w_chan1.shape[1]
        block = 512
        vm, hbm = pl.BlockSpec(memory_space=pltpu.VMEM), pl.BlockSpec(memory_space=pl.ANY)
        act_shape = jax.ShapeDtypeStruct(act_loc.shape, BF16)
        stage = jax.ShapeDtypeStruct((own, n, rows, chans), BF16)
        dma = pltpu.SemaphoreType.DMA
        flops = 12 * own * patches * chans * (hid + hid_tok)
        outs = pl.pallas_call(
            functools.partial(layer_kernel, n),
            out_shape=(act_shape, act_shape, jax.ShapeDtypeStruct((chans, hid), F32), jax.ShapeDtypeStruct((chans, hid), F32),
                       jax.ShapeDtypeStruct((patches, hid_tok), F32), jax.ShapeDtypeStruct((hid_tok, patches), F32),
                       stage, stage, stage, stage),
            in_specs=[hbm, hbm] + [vm] * 12 + [hbm, hbm, vm],
            out_specs=(hbm, hbm, hbm, hbm, vm, vm, hbm, hbm, hbm, hbm),
            scratch_shapes=[
                pltpu.VMEM((2, patches, chans), BF16), pltpu.VMEM((patches, chans), BF16),
                pltpu.VMEM((patches, chans), BF16), pltpu.VMEM((patches, chans), BF16),
                pltpu.VMEM((hid_tok, chans), BF16), pltpu.VMEM((hid_tok, chans), BF16),
                pltpu.VMEM((patches, chans), BF16), pltpu.VMEM((patches, chans), BF16),
                pltpu.VMEM((patches, chans), F32), pltpu.VMEM((patches, chans), F32),
                pltpu.VMEM((patches, block), BF16), pltpu.VMEM((patches, block), BF16),
                pltpu.VMEM((2, chans, block), BF16), pltpu.VMEM((2, block, chans), BF16),
                pltpu.VMEM((3, chans, block), F32), pltpu.VMEM((3, chans, block), F32),
                dma((2,)), dma((2,)), dma((own,)), dma((own,)), dma((1,)), dma((1,)),
                dma((2,)), dma, dma((2,)), dma((2,)), dma((2, 2)), dma((2, 3)), dma((2, 3)),
            ],
            compiler_params=pltpu.CompilerParams(
                collective_id=0, has_side_effects=True, vmem_limit_bytes=67_000_000),
            cost_estimate=pl.CostEstimate(flops=flops, bytes_accessed=10 * act_loc.size, transcendentals=0),
        )(act_loc, grad_loc, ln1_scale[None], ln1_shift[None], ln2_scale[None], ln2_shift[None], b_tok1[:, None],
          b_tok2[:, None], b_chan1[None], b_chan2[None], w_tok1, w_tok1.T, w_tok2, w_tok2.T, w_chan1, w_chan2,
          jnp.eye(256, dtype=BF16))
        act_out, grad_in, dw1, dw2_t, dwt1, dwt2 = outs[:6]
        grads = lax.psum((dwt1, dwt2, dw1, dw2_t.T), "seq")
        return (act_out, grad_in) + tuple(grads)

    return jax.shard_map(device_step, mesh=mesh, in_specs=spec_in, out_specs=spec_out, check_vma=False)
```

time: 1970 us -> 1400 us (0.71)
  Pallas kernels: 0 us -> 948 us
  matrix products: 681 us -> 0 us
  blocking collectives: 379 us -> 0 us
  local copies, waits for them, and re-layouts: 365 us -> 65.1 us
  other arithmetic: 155 us -> 0.68 us
  waiting for transfers between devices: 350 us -> 374 us
    pallas_call x0 -> x1, Pallas kernels: none -> 948 us  [device_step(): pl.pallas_call(functools.partial(layer_kernel, n), out_shape=(act_shape,...]
    dot_general x12 -> x0, matrix products: 681 us -> none  [the longest x1 150 us: device_step(): jnp.einsum('bsc,hc->bsh', grad_loc, w_chan2, preferred_element_type=jnp.f...]
    all_to_all x2 -> x0, blocking collectives: 379 us -> none  [the longest x1 190 us: device_step(): normed_cols = lax.all_to_all(normed, 'seq', 2, 1, tiled=True)]
    psum x1, waiting for transfers between devices: 155 us -> 374 us  [device_step(): grads = lax.psum((dwt1, dwt2, dw1, dw2_t.T), 'seq')]
    convert_element_type x7 -> x0, local copies, waits for them, and re-layouts: 197 us -> none  [the longest x3 79.9 us: layer_norm(): (centered * lax.rsqrt(row_var + LN_EPS) * ln_scale + ln_shift).astype(jnp...]
    all_to_all x2 -> x0, waiting for transfers between devices: 194 us -> none  [the longest x1 176 us: device_step(): grad_normed = lax.all_to_all(grad_normed_cols, 'seq', 1, 2, tiled=True)]
    all_to_all x4 -> x0, local copies, waits for them, and re-layouts: 105 us -> none  [the longest x2 61.2 us: device_step(): normed_cols = lax.all_to_all(normed, 'seq', 2, 1, tiled=True)]
    reduce_sum x7 -> x0, other arithmetic: 90.9 us -> none  [the longest x2 29.9 us: layer_norm(): centered = widened - row_mean]
  transfers between devices with their start and end apart: 3 -> 1, of which waited for: 3 -> 1; matrix products, arithmetic and copies ran while one was open for 19% -> 0% of each run, Pallas kernels for 0% -> 0%
where the time goes in v1:
time: 1400 us
  Pallas kernels  948 us (68%)
  waiting for transfers between devices  374 us (27%)
  local copies, waits for them, and re-layouts  65.1 us (5%)
  between operations  14.1 us (1%)
    pallas_call x1, Pallas kernels, device_step(): pl.pallas_call(functools.partial(layer_kernel, n), out_shape=(act_shape,...  948 us
    psum x1, waiting for transfers between devices, device_step(): grads = lax.psum((dwt1, dwt2, dw1, dw2_t.T), 'seq')  374 us
    unnamed x20, local copies, waits for them, and re-layouts  61.9 us
  transfers between devices with their start and end apart: 1, of which 1 were waited for; matrix products, arithmetic and copies ran while one was open for 0% of the time, Pallas kernels for 0%

profile of v1, /device:TPU:112, one launch (start us, length us, event | category | flops | bytes accessed | tf_op | source)
XLA Modules:
  0.0 1402.0 jit_solution(5164353341766732637)
XLA Ops:
  7.2 0.1 all-reduce.3.cloned.1.call-start
  7.2 0.7 fusion.eye
  7.9 1.5 copy.25.bt1
  9.5 1.7 copy.26.bt2
  11.2 2.3 copy.23
  13.4 2.3 copy.24
  15.7 947.7 %shard_map.181 = (bf16[64,128,1024]{2,1,0:T(8,128)(2,1)}, bf16[64,128,1024]{2,1,0:T(8,128)(2,1)}, f32[1024,4096]{1,0:T(8,128)}, f32[1024,4096]{1,0:T(8,128)}, f3...) custom-call(bf16[64,128,1024]{2,1,0:T(8,128)(2,1)} %x_hbm.1, ...), custom_call_target="tpu_custom_call" | custom-call | flops 463856467968 | bytes 83886080 | tf_op jit(solution)/shard_map/pallas_call | solution.py:346
  963.4 0.1 all-reduce.3.cloned.1.call-update
  963.5 374.2 %all-reduce.3.cloned.1.call-done = (f32[1024,512]{1,0:T(8,128)}, f32[512,1024]{1,0:T(8,128)}, f32[1024,4096]{1,0:T(8,128)}, f32[4096,1024]{0,1:T(8,128)}) async-done(((f32[1024,512]{1,0:T(8,128)}, f32[512,1024]{1,0:T(8,128)}, f32[1024,4096]{1,0:T(8,128)}, f32[4096,1024]{0,1:T(8,128)}), (f32[1024,512]{1,0:T(8,128)}, f32[512,1024]{1,0:T(8,128)}, f32[1024,4096]{1,0:T(8,128)}, ...) | async-done | bytes 37748752 | tf_op jit(solution)/shard_map/psum | solution.py:372
  1337.7 17.4 %copy.27 = f32[4096,1024]{1,0:T(8,128)} copy(f32[4096,1024]{0,1:T(8,128)} %get-tuple-element.33) | data formatting | bytes 33554432
  1355.1 0.0 slice-start
  1355.1 0.0 slice-start.1
  1355.1 15.2 %copy.37 = bf16[64,128,1024]{2,1,0:T(8,128)(2,1)} copy(bf16[64,128,1024]{2,1,0:T(8,128)(2,1)} %get-tuple-element.40) | data formatting | bytes 33554432
  1370.4 0.0 copy-start.1
  1370.4 0.0 copy-start
  1370.4 0.0 slice-start.2
  1370.4 0.0 slice-start.3
  1370.4 15.9 %copy.38 = bf16[64,128,1024]{2,1,0:T(8,128)(2,1)} copy(bf16[64,128,1024]{2,1,0:T(8,128)(2,1)} %get-tuple-element.41) | data formatting | bytes 33554432
  1386.3 0.0 copy-done.1
  1386.3 1.3 copy.39
  1387.6 0.0 copy-done
  1387.6 1.3 copy.40
  1388.9 0.0 slice-done
  1388.9 0.0 slice-done.1
  1388.9 0.0 slice-done.2
  1388.9 0.0 slice-done.3
  1388.9 6.2 copy.41
  (1 shorter events, 0.0 us)
Async XLA Ops:
  7.2 1330.5 %all-reduce.3.cloned.1.call-start = ((), (), s32[]{:S(2)}) async-start(), calls=%async_computation | async-start | bytes 75497472 | tf_op jit(solution)/shard_map/psum | solution.py:372
  1355.1 33.8 %slice-start = ((s8[16777216]{0:T(1024)(128)(4,1)}), s8[4194304]{0:T(1024)(128)(4,1)S(1)}, s32[]{:S(2)}) async-start(s8[16777216]{0:T(1024)(128)(4,1)} %bitcast.12), calls=%async_computation.1 | async-start | bytes 8388608
  1355.1 33.8 %slice-start.1 = ((s8[16777216]{0:T(1024)(128)(4,1)}), s8[4194304]{0:T(1024)(128)(4,1)S(1)}, s32[]{:S(2)}) async-start(s8[16777216]{0:T(1024)(128)(4,1)} %bitcast.12), calls=%async_computation.2 | async-start | bytes 8388608
  1370.4 15.9 %copy-start.1 = (f32[1024,512]{1,0:T(8,128)S(1)}, f32[1024,512]{1,0:T(8,128)}, u32[]{:S(2)}) copy-start(f32[1024,512]{1,0:T(8,128)} %get-tuple-element.42) | copy-start | bytes 6291460
  1370.4 17.2 %copy-start = (f32[512,1024]{1,0:T(8,128)S(1)}, f32[512,1024]{1,0:T(8,128)}, u32[]{:S(2)}) copy-start(f32[512,1024]{1,0:T(8,128)} %get-tuple-element.43) | copy-start | bytes 6291460
  1370.4 18.5 %slice-start.2 = ((s8[16777216]{0:T(1024)(128)(4,1)}), s8[4194304]{0:T(1024)(128)(4,1)S(1)}, s32[]{:S(2)}) async-start(s8[16777216]{0:T(1024)(128)(4,1)} %bitcast.12), calls=%async_computation.3 | async-start | bytes 8388608
  1370.4 18.5 %slice-start.3 = ((s8[16777216]{0:T(1024)(128)(4,1)}), s8[4194304]{0:T(1024)(128)(4,1)S(1)}, s32[]{:S(2)}) async-start(s8[16777216]{0:T(1024)(128)(4,1)} %bitcast.12), calls=%async_computation.4 | async-start | bytes 8388608
Sparse Core Ops, SparseCore 0:
  963.6 374.0 all-reduce.2
